TPU v7x, 128 devices: a whole 4x4x4 slice. The times are simulated.
128 devices in a mesh: dom: 32 (over y, x, core), dim: 4 (over z).
Axes of the slice: x: 4, y: 4, z: 4, core: 2. Of those that a mesh axis runs over, the one named last changes fastest.
Arguments:
- particles: float32 [256, 1024], P('dom', 'dim'), may hold values from -5 to 5
- data_rows: bfloat16 [256, 16, 1024], P('dom', None, 'dim'), may hold values from -0.375 to 0.375
- labels: int32 [256, 16], P('dom'), may hold values from 0 to 1
Outputs:
- updates: float32 [2, 256, 1024], P(None, 'dom', 'dim')
All inputs are finite; a program needn't handle non-finite values.
Results may differ from a plain program's by a relative error of at most 0.0003.
Values may be sent and summed in bfloat16 or wider, within the bound.
No kernel may reach another device: no remote copies, remote signals or barrier semaphores. Data moves between devices by JAX's collectives and lax.ppermute only.
A program may use at most 64 MiB of HBM per device.

v0:
```python
from functools import partial
import jax
import jax.numpy as jnp
from jax import lax
from jax.sharding import Mesh
from jax.sharding import PartitionSpec as P

NEWTON = 2
CG_STEPS = 2
BAND = 1
DOM_DIM = ("dom_0", "dom_1", "dom_2", "dim")
DOM = ("dom_0", "dom_1", "dom_2")
prior_precision = 0.05
like_weight = 4.0
move_size = 0.5
highest = lax.Precision.HIGHEST


def by_axis(x, axes):
    for axis in axes:
        x = lax.psum(x, axis)
    return x


def laid_out(blocks, dim):
    blocks = jnp.moveaxis(blocks, 0, dim)
    shape = blocks.shape
    return blocks.reshape(*shape[:dim], shape[dim] * shape[dim + 1], *shape[dim + 2 :])


def from_everyone(x, axis):
    copies = jnp.broadcast_to(x, (lax.axis_size(axis), *x.shape))
    return lax.all_to_all(copies, axis, split_axis=0, concat_axis=0, tiled=True)


def gathered_copies(x, axis, dim):
    return laid_out(from_everyone(x, axis), dim)


def side_by_side(arrays, axis, dim, along):
    both = jnp.concatenate(arrays, axis=along)
    filled, at, outs = (lax.all_gather(both, axis, axis=dim, tiled=True), 0, [])
    for a in arrays:
        outs.append(lax.slice_in_dim(filled, at, at + a.shape[along], axis=along))
        at += a.shape[along]
    return tuple(outs)


def taken_together(x, axis):
    return from_everyone(x, axis).sum(axis=0)


def packed_total(arrays, axis):
    ends = [0]
    for a in arrays:
        ends.append(ends[-1] + a.size)
    total = taken_together(jnp.concatenate([a.ravel() for a in arrays]), axis)
    return tuple((total[b:e].reshape(a.shape) for a, b, e in zip(arrays, ends, ends[1:])))


def split_up(x, dim, size):
    shape = x.shape
    blocks = x.reshape(*shape[:dim], size, shape[dim] // size, *shape[dim + 1 :])
    return jnp.moveaxis(blocks, dim, 0)


def sum_at_owner(x, axis, dim):
    blocks = split_up(x, dim, lax.axis_size(axis))
    arrived = lax.all_to_all(blocks, axis, split_axis=0, concat_axis=0, tiled=True)
    return arrived.sum(axis=0)


def drift_terms(x_local, squares, kernel_scale, rows_pos, rows_grad):
    inner_rows = jnp.einsum("id,jd->ij", x_local, rows_pos, precision=highest)
    row_squares = jnp.sum(rows_pos * rows_pos, axis=1)
    distance = squares[:, None] + row_squares[None, :] - 2.0 * inner_rows
    kernel = jnp.exp(-distance / kernel_scale)
    kernel_sq = kernel * kernel
    kernel_grad = jnp.dot(kernel, rows_grad, precision=highest)
    kernel_pos = jnp.dot(kernel, rows_pos, precision=highest)
    square_pos = jnp.dot(kernel_sq, rows_pos, precision=highest)
    return (
        kernel,
        kernel_grad,
        kernel_pos,
        square_pos,
        jnp.sum(kernel, axis=1),
        jnp.sum(kernel_sq, axis=1),
    )


def pair_block(running, piece, start, kernel, curve_rows, pos_rows, vectors, cross_scale):
    weight_sq = (kernel * kernel).T
    factor_part = piece.astype(jnp.float32)
    projected = jnp.einsum("jrd,id->jri", factor_part, vectors, precision=highest)
    weighted = projected * curve_rows[:, :, None] * weight_sq[:, None, :]
    running = jnp.einsum("jrd,jri->id", factor_part, weighted, precision=highest)
    along_pair = jnp.einsum("jd,id->ji", pos_rows, vectors, precision=highest)
    return running + cross_scale * jnp.einsum(
        "ji,jd->id", weight_sq * along_pair, pos_rows, precision=highest
    )


def residual_sum(vectors):
    return by_axis(jnp.sum(vectors * vectors), DOM_DIM)


def per_device(particles, data_rows, labels):
    dim_count = lax.axis_size("dim")
    dom_count = lax.axis_size(DOM)
    part_rows = particles.shape[0]
    slice_width = particles.shape[1]
    width = slice_width * dim_count
    quarter = part_rows // dim_count
    total_count = part_rows * dom_count
    kernel_scale = 1.0 * BAND * width
    cross_scale = 4.0 / (kernel_scale * kernel_scale)
    lane = lax.axis_index("dim")
    first_row = lane * quarter
    first_col = lane * slice_width
    own_factors = lax.all_to_all(data_rows, "dim", split_axis=0, concat_axis=2, tiled=True)
    factor_float = own_factors.astype(jnp.float32)
    own_targets = lax.dynamic_slice_in_dim(labels, first_row, quarter, 0).astype(jnp.float32)
    current = particles
    outputs = []
    for newton_step in range(NEWTON):
        x_local = gathered_copies(current, "dim", 1)
        own_pos = lax.dynamic_slice_in_dim(x_local, first_row, quarter, 0)
        logits = jnp.einsum("jrd,jd->jr", factor_float, own_pos, precision=highest)
        probs = jax.nn.sigmoid(logits)
        own_grad = -prior_precision * own_pos + like_weight * jnp.einsum(
            "jr,jrd->jd", own_targets - probs, factor_float, precision=highest
        )
        own_curve = like_weight * probs * (1.0 - probs)
        pos_rows, grad_rows, curve_rows = side_by_side((own_pos, own_grad, own_curve), DOM, 0, 1)
        squares = jnp.sum(x_local * x_local, axis=1)
        kernel, kernel_grad, kernel_pos, square_pos, kernel_total, square_total = drift_terms(
            x_local, squares, kernel_scale, pos_rows, grad_rows
        )
        kernel_grad, kernel_pos, square_pos, kernel_total, square_total = packed_total(
            (kernel_grad, kernel_pos, square_pos, kernel_total, square_total), "dim"
        )
        drift_full = (
            kernel_grad + 2.0 / kernel_scale * (x_local * kernel_total[:, None] - kernel_pos)
        ) / total_count
        drift = lax.dynamic_slice_in_dim(drift_full, first_col, slice_width, 1)
        mean_slice = lax.dynamic_slice_in_dim(square_pos, first_col, slice_width, 1)
        solution = jnp.zeros_like(drift)
        residual = drift
        direction = drift
        norm_now = residual_sum(residual)
        for solve_step in range(CG_STEPS):
            vectors_full = gathered_copies(direction, "dim", 1)
            start_total = jnp.zeros((part_rows, width), jnp.float32)
            block_step = partial(
                pair_block,
                kernel=kernel,
                curve_rows=curve_rows,
                pos_rows=pos_rows,
                vectors=vectors_full,
                cross_scale=cross_scale,
            )
            pairs = block_step(start_total, gathered_copies(own_factors, DOM, 0), jnp.int32(0))
            pairs = sum_at_owner(pairs, "dim", 1)
            along_self = jnp.sum(x_local * vectors_full, axis=1)
            along_mean = jnp.sum(vectors_full * square_pos, axis=1)
            local = prior_precision * square_total[:, None] * direction + cross_scale * (
                current * (along_self * square_total - along_mean)[:, None]
                - along_self[:, None] * mean_slice
            )
            image = (pairs + local) / total_count
            curve_total, mixed_total, image_square = (
                by_axis(jnp.sum(direction * image), DOM_DIM),
                by_axis(jnp.sum(residual * image), DOM_DIM),
                by_axis(jnp.sum(image * image), DOM_DIM),
            )
            alpha = norm_now / curve_total
            norm_next = norm_now - 2.0 * alpha * mixed_total + alpha * alpha * image_square
            solution = solution + alpha * direction
            residual = residual - alpha * image
            if solve_step + 1 < CG_STEPS:
                direction = residual + norm_next / norm_now * direction
                norm_now = norm_next
        outputs.append(solution)
        current = current + move_size * solution
    return jnp.stack(outputs)


def solution(mesh):
    torus = Mesh(
        mesh.devices.reshape(4, 4, 2, mesh.shape["dim"]), ("dom_0", "dom_1", "dom_2", "dim")
    )
    in_specs = (P(DOM, "dim"), P(DOM, None, "dim"), P(DOM, None))
    out_specs = P(None, DOM, "dim")
    return jax.shard_map(
        per_device, mesh=torus, in_specs=in_specs, out_specs=out_specs, check_vma=False
    )
```

profile of v0, /device:TPU:2, one launch (start us, length us, event | category | flops | bytes accessed | tf_op | source)
XLA Modules:
  0.0 380.4 jit_solution(8490471881135553122)
XLA Ops:
  6.6 5.5 %all-to-all-done = f32[4,8,256]{2,1,0:T(8,128)S(1)} async-done(((f32[4,8,256]{2,1,0:T(8,128)}), f32[4,8,256]{2,1,0:T(8,128)S(1)}, u32[]{:S(2)}, u32[]{:S(2)}) %all-to-all-start) | async-done | bytes 32800 | tf_op jit(solution)/shard_map/all_to_all | solution.py:33
  15.6 5.4 %all-to-all-done.1 = bf16[8,16,256]{2,1,0:T(8,128)(2,1)S(1)} async-done(((bf16[8,16,256]{2,1,0:T(8,128)(2,1)}), bf16[8,16,256]{2,1,0:T(8,128)(2,1)S(1)}, u32[]{:S(2)}, u32[]{:S(2)}) %all-to-all-start.1) | async-done | bytes 65568 | tf_op jit(solution)/shard_map/all_to_all | solution.py:121
  22.1 24.9 %all-gather = f32[32,2,2064]{2,1,0:T(2,128)S(1)} all-gather(f32[1,2,2064]{2,1,0:T(2,128)S(1)} %maximum_bitcast_fusion), channel_id=1, replica_groups=mesh['dom_0'=4,'dom_1'=4,'dom_2'=2,'dim'=4] {'dom_0','dom_1','dom_2'}, dimensions={0}, use_global_device_ids=true | all-gather | bytes 544896 | tf_op jit(solution)/shard_map/all_gather | solution.py:42
  53.4 8.9 %all-to-all-done.2 = f32[4,1,24592]{2,1,0:T(1,128)S(1)} async-done(((f32[4,1,24592]{2,1,0:T(1,128)}), f32[4,1,24592]{2,1,0:T(1,128)S(1)}, u32[]{:S(2)}, u32[]{:S(2)}) %all-to-all-start.2) | async-done | bytes 393504 | tf_op jit(solution)/shard_map/all_to_all | solution.py:33
  75.3 5.8 %all-to-all-start.4 = ((bf16[32,2,16,1024]{3,1,2,0:T(2,128)(2,1)}), bf16[32,2,16,1024]{3,1,2,0:T(2,128)(2,1)S(1)}, u32[]{:S(2)}, u32[]{:S(2)}) async-start(bf16[32,2,16,1024]{3,1,2,0:T(2,128)(2,1)} %broadcast_in_dim.21), calls=%async_computation.4 | async-start | bytes 4194304 | tf_op jit(solution)/shard_map/all_to_all | solution.py:33
  81.7 27.2 %all-to-all-done.4 = bf16[32,2,16,1024]{3,1,2,0:T(2,128)(2,1)S(1)} async-done(((bf16[32,2,16,1024]{3,1,2,0:T(2,128)(2,1)}), bf16[32,2,16,1024]{3,1,2,0:T(2,128)(2,1)S(1)}, u32[]{:S(2)}, u32[]{:S(2)}) %all-to-all-start.4) | async-done | bytes 2097184 | tf_op jit(solution)/shard_map/all_to_all | solution.py:33
  122.8 5.3 %all-to-all-done.5 = f32[4,8,256]{2,1,0:T(8,128)S(1)} async-done(((f32[4,8,256]{2,1,0:T(8,128)}), f32[4,8,256]{2,1,0:T(8,128)S(1)}, u32[]{:S(2)}, u32[]{:S(2)}) %all-to-all-start.5) | async-done | bytes 32800 | tf_op jit(solution)/shard_map/all_to_all | solution.py:69
  128.9 8.9 %all-reduce.5 = (f32[]{:T(128)}, f32[]{:T(128)}, f32[]{:T(128)}) all-reduce(f32[]{:T(128)} %get-tuple-element.18, f32[]{:T(128)} %get-tuple-element.17, f32[]{:T(128)} %get-tuple-element.16), channel_id=1, replica_groups=mesh['dom_0'=4,'dom_1'=4,'dom_2'=2,'dim'=4] {'dom_0'}, use_global_device_ids=true, to_apply=%region_6.0 | all-reduce | flops 3 | bytes 24 | tf_op jit(solution)/shard_map/psum | solution.py:21
  137.9 10.3 %all-reduce.3 = (f32[]{:T(128)}, f32[]{:T(128)}, f32[]{:T(128)}) all-reduce(f32[]{:T(128)} %get-tuple-element.38, f32[]{:T(128)} %get-tuple-element.39, f32[]{:T(128)} %get-tuple-element.40), channel_id=1, replica_groups=mesh['dom_0'=4,'dom_1'=4,'dom_2'=2,'dim'=4] {'dom_1'}, use_global_device_ids=true, to_apply=%region_7.0 | all-reduce | flops 3 | bytes 24 | tf_op jit(solution)/shard_map/psum | solution.py:21
  151.3 9.6 %all-reduce.1 = (f32[]{:T(128)}, f32[]{:T(128)}, f32[]{:T(128)}) all-reduce(f32[]{:T(128)} %get-tuple-element.44, f32[]{:T(128)} %get-tuple-element.45, f32[]{:T(128)} %get-tuple-element.46), channel_id=1, replica_groups=mesh['dom_0'=4,'dom_1'=4,'dom_2'=2,'dim'=4] {'dim'}, use_global_device_ids=true, to_apply=%region_9.0 | all-reduce | flops 3 | bytes 24 | tf_op jit(solution)/shard_map/psum | solution.py:21
  164.8 7.8 %all_to_all.88 = f32[4,8,256]{2,1,0:T(8,128)S(1)} all-to-all(f32[4,8,256]{2,1,0:T(8,128)S(1)} %broadcast_in_dim.22), channel_id=1, replica_groups=mesh['dom_0'=4,'dom_1'=4,'dom_2'=2,'dim'=4] {'dim'}, dimensions={0} | all-to-all | bytes 65536 | tf_op jit(solution)/shard_map/all_to_all | solution.py:33
  186.8 10.3 %psum.260 = f32[]{:T(128)} all-reduce(f32[]{:T(128)} %multiply_reduce_fusion.10), channel_id=1, replica_groups=mesh['dom_0'=4,'dom_1'=4,'dom_2'=2,'dim'=4] {'dom_0'}, use_global_device_ids=true, to_apply=%region_27.0 | all-reduce | flops 1 | bytes 8 | tf_op jit(solution)/shard_map/psum | solution.py:21
  197.1 8.3 %psum.261 = f32[]{:T(128)} all-reduce(f32[]{:T(128)} %psum.260), channel_id=1, replica_groups=mesh['dom_0'=4,'dom_1'=4,'dom_2'=2,'dim'=4] {'dom_1'}, use_global_device_ids=true, to_apply=%region_28.0 | all-reduce | flops 1 | bytes 8 | tf_op jit(solution)/shard_map/psum | solution.py:21
  208.5 9.5 %psum.263 = f32[]{:T(128)} all-reduce(f32[]{:T(128)} %psum.262), channel_id=1, replica_groups=mesh['dom_0'=4,'dom_1'=4,'dom_2'=2,'dim'=4] {'dim'}, use_global_device_ids=true, to_apply=%region_30.0 | all-reduce | flops 1 | bytes 8 | tf_op jit(solution)/shard_map/psum | solution.py:21
  218.7 7.8 %all_to_all.89 = f32[4,8,256]{2,1,0:T(8,128)S(1)} all-to-all(f32[4,8,256]{2,1,0:T(8,128)S(1)} %broadcast_in_dim.23), channel_id=1, replica_groups=mesh['dom_0'=4,'dom_1'=4,'dom_2'=2,'dim'=4] {'dim'}, dimensions={0} | all-to-all | bytes 65536 | tf_op jit(solution)/shard_map/all_to_all | solution.py:33
  227.7 23.8 %all-gather.1 = f32[32,2,2064]{2,1,0:T(2,128)S(1)} all-gather(f32[1,2,2064]{2,1,0:T(2,128)S(1)} %maximum_bitcast_fusion.1), channel_id=1, replica_groups=mesh['dom_0'=4,'dom_1'=4,'dom_2'=2,'dim'=4] {'dom_0','dom_1','dom_2'}, dimensions={0}, use_global_device_ids=true | all-gather | bytes 544896 | tf_op jit(solution)/shard_map/all_gather | solution.py:42
  253.8 11.4 %all_to_all.90 = f32[4,1,24592]{2,1,0:T(1,128)S(1)} all-to-all(f32[4,1,24592]{2,1,0:T(1,128)S(1)} %broadcast_in_dim.24), channel_id=1, replica_groups=mesh['dom_0'=4,'dom_1'=4,'dom_2'=2,'dim'=4] {'dim'}, dimensions={0} | all-to-all | bytes 786944 | tf_op jit(solution)/shard_map/all_to_all | solution.py:33
  289.2 9.6 %all-reduce.4 = (f32[]{:T(128)}, f32[]{:T(128)}, f32[]{:T(128)}) all-reduce(f32[]{:T(128)} %get-tuple-element.15, f32[]{:T(128)} %get-tuple-element.14, f32[]{:T(128)} %get-tuple-element.13), channel_id=1, replica_groups=mesh['dom_0'=4,'dom_1'=4,'dom_2'=2,'dim'=4] {'dom_0'}, use_global_device_ids=true, to_apply=%region_37.0 | all-reduce | flops 3 | bytes 24 | tf_op jit(solution)/shard_map/psum | solution.py:21
  298.8 10.5 %all-reduce.2 = (f32[]{:T(128)}, f32[]{:T(128)}, f32[]{:T(128)}) all-reduce(f32[]{:T(128)} %get-tuple-element.35, f32[]{:T(128)} %get-tuple-element.36, f32[]{:T(128)} %get-tuple-element.37), channel_id=1, replica_groups=mesh['dom_0'=4,'dom_1'=4,'dom_2'=2,'dim'=4] {'dom_1'}, use_global_device_ids=true, to_apply=%region_38.0 | all-reduce | flops 3 | bytes 24 | tf_op jit(solution)/shard_map/psum | solution.py:21
  312.4 9.6 %all-reduce = (f32[]{:T(128)}, f32[]{:T(128)}, f32[]{:T(128)}) all-reduce(f32[]{:T(128)} %get-tuple-element.41, f32[]{:T(128)} %get-tuple-element.42, f32[]{:T(128)} %get-tuple-element.43), channel_id=1, replica_groups=mesh['dom_0'=4,'dom_1'=4,'dom_2'=2,'dim'=4] {'dim'}, use_global_device_ids=true, to_apply=%region_40.0 | all-reduce | flops 3 | bytes 24 | tf_op jit(solution)/shard_map/psum | solution.py:21
  325.9 7.8 %all_to_all.91 = f32[4,8,256]{2,1,0:T(8,128)S(1)} all-to-all(f32[4,8,256]{2,1,0:T(8,128)S(1)} %broadcast_in_dim.26), channel_id=1, replica_groups=mesh['dom_0'=4,'dom_1'=4,'dom_2'=2,'dim'=4] {'dim'}, dimensions={0} | all-to-all | bytes 65536 | tf_op jit(solution)/shard_map/all_to_all | solution.py:33
  347.8 8.3 %psum.276 = f32[]{:T(128)} all-reduce(f32[]{:T(128)} %multiply_reduce_fusion.6), channel_id=1, replica_groups=mesh['dom_0'=4,'dom_1'=4,'dom_2'=2,'dim'=4] {'dom_0'}, use_global_device_ids=true, to_apply=%region_58.0 | all-reduce | flops 1 | bytes 8 | tf_op jit(solution)/shard_map/psum | solution.py:21
  356.2 10.4 %psum.277 = f32[]{:T(128)} all-reduce(f32[]{:T(128)} %psum.276), channel_id=1, replica_groups=mesh['dom_0'=4,'dom_1'=4,'dom_2'=2,'dim'=4] {'dom_1'}, use_global_device_ids=true, to_apply=%region_59.0 | all-reduce | flops 1 | bytes 8 | tf_op jit(solution)/shard_map/psum | solution.py:21
  369.6 9.5 %psum.279 = f32[]{:T(128)} all-reduce(f32[]{:T(128)} %psum.278), channel_id=1, replica_groups=mesh['dom_0'=4,'dom_1'=4,'dom_2'=2,'dim'=4] {'dim'}, use_global_device_ids=true, to_apply=%region_61.0 | all-reduce | flops 1 | bytes 8 | tf_op jit(solution)/shard_map/psum | solution.py:21
  (146 shorter events, 114.5 us)
Async XLA Ops:
  1.3 10.8 %all-to-all-start = ((f32[4,8,256]{2,1,0:T(8,128)}), f32[4,8,256]{2,1,0:T(8,128)S(1)}, u32[]{:S(2)}, u32[]{:S(2)}) async-start(f32[4,8,256]{2,1,0:T(8,128)} %broadcast_in_dim.18), calls=%async_computation | async-start | bytes 65536 | tf_op jit(solution)/shard_map/all_to_all | solution.py:33
  12.1 8.9 %all-to-all-start.1 = ((bf16[8,16,256]{2,1,0:T(8,128)(2,1)}), bf16[8,16,256]{2,1,0:T(8,128)(2,1)S(1)}, u32[]{:S(2)}, u32[]{:S(2)}) async-start(bf16[8,16,256]{2,1,0:T(8,128)(2,1)} %param.4), calls=%async_computation.1 | async-start | bytes 131072 | tf_op jit(solution)/shard_map/all_to_all | solution.py:121
  49.9 12.3 %all-to-all-start.2 = ((f32[4,1,24592]{2,1,0:T(1,128)}), f32[4,1,24592]{2,1,0:T(1,128)S(1)}, u32[]{:S(2)}, u32[]{:S(2)}) async-start(f32[4,1,24592]{2,1,0:T(1,128)} %broadcast_in_dim.19), calls=%async_computation.2 | async-start | bytes 790528 | tf_op jit(solution)/shard_map/all_to_all | solution.py:33
  63.3 8.7 %all-to-all-start.3 = ((f32[4,8,256]{2,1,0:T(8,128)}), f32[4,8,256]{2,1,0:T(8,128)S(1)}, u32[]{:S(2)}, u32[]{:S(2)}) async-start(f32[4,8,256]{2,1,0:T(8,128)} %broadcast_in_dim.20), calls=%async_computation.3 | async-start | bytes 65536 | tf_op jit(solution)/shard_map/all_to_all | solution.py:33
  75.3 33.7 %all-to-all-start.4 = ((bf16[32,2,16,1024]{3,1,2,0:T(2,128)(2,1)}), bf16[32,2,16,1024]{3,1,2,0:T(2,128)(2,1)S(1)}, u32[]{:S(2)}, u32[]{:S(2)}) async-start(bf16[32,2,16,1024]{3,1,2,0:T(2,128)(2,1)} %broadcast_in_dim.21), calls=%async_computation.4 | async-start | bytes 4194304 | tf_op jit(solution)/shard_map/all_to_all | solution.py:33
  115.1 13.1 %copy-start = (f32[8,256]{1,0:T(8,128)S(1)}, f32[8,256]{1,0:T(8,128)}, u32[]{:S(2)}) copy-start(f32[8,256]{1,0:T(8,128)} %param.3) | copy-start | bytes 24580
  119.5 8.7 %all-to-all-start.5 = ((f32[4,8,256]{2,1,0:T(8,128)}), f32[4,8,256]{2,1,0:T(8,128)S(1)}, u32[]{:S(2)}, u32[]{:S(2)}) async-start(f32[4,8,256]{2,1,0:T(8,128)} %bitcast.15), calls=%async_computation.5 | async-start | bytes 65536 | tf_op jit(solution)/shard_map/all_to_all | solution.py:69
  177.4 8.7 %all-to-all-start.7 = ((f32[4,8,256]{2,1,0:T(8,128)}), f32[4,8,256]{2,1,0:T(8,128)S(1)}, u32[]{:S(2)}, u32[]{:S(2)}) async-start(f32[4,8,256]{2,1,0:T(8,128)} %bitcast.20), calls=%async_computation.7 | async-start | bytes 65536 | tf_op jit(solution)/shard_map/all_to_all | solution.py:69
  266.3 8.7 %all-to-all-start.10 = ((f32[4,8,256]{2,1,0:T(8,128)}), f32[4,8,256]{2,1,0:T(8,128)S(1)}, u32[]{:S(2)}, u32[]{:S(2)}) async-start(f32[4,8,256]{2,1,0:T(8,128)} %broadcast_in_dim.25), calls=%async_computation.10 | async-start | bytes 65536 | tf_op jit(solution)/shard_map/all_to_all | solution.py:33
  279.8 8.7 %all-to-all-start.11 = ((f32[4,8,256]{2,1,0:T(8,128)}), f32[4,8,256]{2,1,0:T(8,128)S(1)}, u32[]{:S(2)}, u32[]{:S(2)}) async-start(f32[4,8,256]{2,1,0:T(8,128)} %bitcast.35), calls=%async_computation.11 | async-start | bytes 65536 | tf_op jit(solution)/shard_map/all_to_all | solution.py:69
  338.5 8.7 %all-to-all-start.13 = ((f32[4,8,256]{2,1,0:T(8,128)}), f32[4,8,256]{2,1,0:T(8,128)S(1)}, u32[]{:S(2)}, u32[]{:S(2)}) async-start(f32[4,8,256]{2,1,0:T(8,128)} %bitcast.40), calls=%async_computation.13 | async-start | bytes 65536 | tf_op jit(solution)/shard_map/all_to_all | solution.py:69
where the time goes:
time: 382 us; the launch traced here: 380 us
  blocking collectives  211 us (55%)
  waiting for transfers between devices  78.4 us (21%)
  starting transfers between devices  37.4 us (10%)
  matrix products  21.9 us (6%)
  local copies, waits for them, and re-layouts  14.8 us (4%)
  between operations  9.71 us (3%)
  other arithmetic  7.51 us (2%)
    psum x16, blocking collectives, by_axis(): x = lax.psum(x, axis)  127 us
    all_to_all x5, waiting for transfers between devices, from_everyone(): return lax.all_to_all(copies, axis, split_axis=0, concat_axis=0, tiled=True)  52.1 us
    all_gather x2, blocking collectives, side_by_side(): filled, at, outs = (lax.all_gather(both, axis, axis=dim, tiled=True), 0, [])  48.6 us
    all_to_all x4, blocking collectives, from_everyone(): return lax.all_to_all(copies, axis, split_axis=0, concat_axis=0, tiled=True)  34.8 us
    all_to_all x5, starting transfers between devices, from_everyone(): return lax.all_to_all(copies, axis, split_axis=0, concat_axis=0, tiled=True)  21.1 us
    all_to_all x4, waiting for transfers between devices, sum_at_owner(): lax.all_to_all(blocks, axis, split_axis=0, concat_axis=0, tiled=True)  20.9 us
    all_to_all x4, starting transfers between devices, sum_at_owner(): lax.all_to_all(blocks, axis, split_axis=0, concat_axis=0, tiled=True)  13 us
    dot_general x4, matrix products, pair_block(): jnp.einsum('jrd,id->jri', factor_part, vectors, precision=highest)  10.2 us
  transfers between devices with their start and end apart: 10, of which 10 were waited for; matrix products, arithmetic and copies ran while one was open for 0% of the time, Pallas kernels for 0%

commit v1 on v0

--- a/solution.py
+++ b/solution.py
@@ -18,7 +18,7 @@
 
 def by_axis(x, axes):
     for axis in axes:
-        x = lax.psum(x, axis)
+        x = jnp.sum(lax.all_gather(x, axis), axis=0)
     return x
 
 

time: 382 us -> 438 us (1.15)
  local copies, waits for them, and re-layouts: 14.8 us -> 61.5 us
  other arithmetic: 7.51 us -> 27.3 us
  blocking collectives: 211 us -> 200 us
    psum x16 -> x0, blocking collectives: 127 us -> none  [by_axis(): x = lax.psum(x, axis)]
    unnamed x0 -> x16, blocking collectives: none -> 117 us
    unnamed x16 -> x92, local copies, waits for them, and re-layouts: 0.99 us -> 47.7 us
    reduce_sum x0 -> x32, other arithmetic: none -> 19.8 us  [by_axis(): x = jnp.sum(lax.all_gather(x, axis), axis=0)]
  transfers between devices with their start and end apart: 10 -> 10, of which waited for: 10 -> 10; matrix products, arithmetic and copies ran while one was open for 0% -> 1% of each run, Pallas kernels for 0% -> 0%
where the time goes in v1:
time: 438 us; the launch traced here: 436 us
  blocking collectives  200 us (46%)
  waiting for transfers between devices  77.5 us (18%)
  local copies, waits for them, and re-layouts  61.5 us (14%)
  starting transfers between devices  37.8 us (9%)
  other arithmetic  27.3 us (6%)
  matrix products  22 us (5%)
  between operations  10.2 us (2%)
    unnamed x16, blocking collectives  117 us
    all_to_all x5, waiting for transfers between devices, from_everyone(): return lax.all_to_all(copies, axis, split_axis=0, concat_axis=0, tiled=True)  51.3 us
    all_gather x2, blocking collectives, side_by_side(): filled, at, outs = (lax.all_gather(both, axis, axis=dim, tiled=True), 0, [])  48.6 us
    unnamed x92, local copies, waits for them, and re-layouts  47.7 us
    all_to_all x4, blocking collectives, from_everyone(): return lax.all_to_all(copies, axis, split_axis=0, concat_axis=0, tiled=True)  34.8 us
    all_to_all x5, starting transfers between devices, from_everyone(): return lax.all_to_all(copies, axis, split_axis=0, concat_axis=0, tiled=True)  21.4 us
    all_to_all x4, waiting for transfers between devices, sum_at_owner(): lax.all_to_all(blocks, axis, split_axis=0, concat_axis=0, tiled=True)  20.9 us
    reduce_sum x32, other arithmetic, by_axis(): x = jnp.sum(lax.all_gather(x, axis), axis=0)  19.8 us
  transfers between devices with their start and end apart: 10, of which 10 were waited for; matrix products, arithmetic and copies ran while one was open for 1% of the time, Pallas kernels for 0%

profile of v1, /device:TPU:2, one launch (start us, length us, event | category | flops | bytes accessed | tf_op | source)
XLA Modules:
  0.0 436.3 jit_solution(15447211028113214711)
XLA Ops:
  6.6 5.5 %all-to-all-done = f32[4,8,256]{2,1,0:T(8,128)S(1)} async-done(((f32[4,8,256]{2,1,0:T(8,128)}), f32[4,8,256]{2,1,0:T(8,128)S(1)}, u32[]{:S(2)}, u32[]{:S(2)}) %all-to-all-start) | async-done | bytes 32800 | tf_op jit(solution)/shard_map/all_to_all | solution.py:33
  15.6 5.4 %all-to-all-done.1 = bf16[8,16,256]{2,1,0:T(8,128)(2,1)S(1)} async-done(((bf16[8,16,256]{2,1,0:T(8,128)(2,1)}), bf16[8,16,256]{2,1,0:T(8,128)(2,1)S(1)}, u32[]{:S(2)}, u32[]{:S(2)}) %all-to-all-start.1) | async-done | bytes 65568 | tf_op jit(solution)/shard_map/all_to_all | solution.py:121
  22.1 24.9 %all-gather = f32[32,2,2064]{2,1,0:T(2,128)S(1)} all-gather(f32[1,2,2064]{2,1,0:T(2,128)S(1)} %maximum_bitcast_fusion), channel_id=1, replica_groups=mesh['dom_0'=4,'dom_1'=4,'dom_2'=2,'dim'=4] {'dom_0','dom_1','dom_2'}, dimensions={0}, use_global_device_ids=true | all-gather | bytes 544896 | tf_op jit(solution)/shard_map/all_gather | solution.py:42
  53.4 8.9 %all-to-all-done.2 = f32[4,1,24592]{2,1,0:T(1,128)S(1)} async-done(((f32[4,1,24592]{2,1,0:T(1,128)}), f32[4,1,24592]{2,1,0:T(1,128)S(1)}, u32[]{:S(2)}, u32[]{:S(2)}) %all-to-all-start.2) | async-done | bytes 393504 | tf_op jit(solution)/shard_map/all_to_all | solution.py:33
  75.3 5.9 %all-to-all-start.4 = ((bf16[32,2,16,1024]{3,1,2,0:T(2,128)(2,1)}), bf16[32,2,16,1024]{3,1,2,0:T(2,128)(2,1)S(1)}, u32[]{:S(2)}, u32[]{:S(2)}) async-start(bf16[32,2,16,1024]{3,1,2,0:T(2,128)(2,1)} %broadcast_in_dim.21), calls=%async_computation.4 | async-start | bytes 4194304 | tf_op jit(solution)/shard_map/all_to_all | solution.py:33
  82.5 26.6 %all-to-all-done.4 = bf16[32,2,16,1024]{3,1,2,0:T(2,128)(2,1)S(1)} async-done(((bf16[32,2,16,1024]{3,1,2,0:T(2,128)(2,1)}), bf16[32,2,16,1024]{3,1,2,0:T(2,128)(2,1)S(1)}, u32[]{:S(2)}, u32[]{:S(2)}) %all-to-all-start.4) | async-done | bytes 2097184 | tf_op jit(solution)/shard_map/all_to_all | solution.py:33
  123.0 5.3 %all-to-all-done.5 = f32[4,8,256]{2,1,0:T(8,128)S(1)} async-done(((f32[4,8,256]{2,1,0:T(8,128)}), f32[4,8,256]{2,1,0:T(8,128)S(1)}, u32[]{:S(2)}, u32[]{:S(2)}) %all-to-all-start.5) | async-done | bytes 32800 | tf_op jit(solution)/shard_map/all_to_all | solution.py:69
  133.8 8.2 %all-reduce.37 = (f32[4]{0:T(128)S(1)}, f32[4]{0:T(128)S(1)}, f32[4]{0:T(128)S(1)}) all-reduce(f32[4]{0:T(128)S(1)} %dynamic-update-slice, f32[4]{0:T(128)S(1)} %dynamic-update-slice.4, f32[4]{0:T(128)S(1)} %dynamic-update-slice.8), channel_id=1, replica_groups=mesh['dom_0'=4,'dom_1'=4,'dom_2'=2,'dim'=4] {'dom_0'}, use_global_device_ids=true, to_apply=%add | all-reduce | flops 12 | bytes 96
  148.9 9.6 %all-reduce.35 = (f32[4]{0:T(128)S(1)}, f32[4]{0:T(128)S(1)}, f32[4]{0:T(128)S(1)}) all-reduce(f32[4]{0:T(128)S(1)} %dynamic-update-slice.1, f32[4]{0:T(128)S(1)} %dynamic-update-slice.5, f32[4]{0:T(128)S(1)} %dynamic-update-slice.9), channel_id=1, replica_groups=mesh['dom_0'=4,'dom_1'=4,'dom_2'=2,'dim'=4] {'dom_1'}, use_global_device_ids=true, to_apply=%add.1 | all-reduce | flops 12 | bytes 96
  173.7 8.9 %all-reduce.33 = (f32[4]{0:T(128)S(1)}, f32[4]{0:T(128)S(1)}, f32[4]{0:T(128)S(1)}) all-reduce(f32[4]{0:T(128)S(1)} %dynamic-update-slice.3, f32[4]{0:T(128)S(1)} %dynamic-update-slice.7, f32[4]{0:T(128)S(1)} %dynamic-update-slice.11), channel_id=1, replica_groups=mesh['dom_0'=4,'dom_1'=4,'dom_2'=2,'dim'=4] {'dim'}, use_global_device_ids=true, to_apply=%add.3 | all-reduce | flops 12 | bytes 96
  188.6 7.8 %all_to_all.89 = f32[4,8,256]{2,1,0:T(8,128)S(1)} all-to-all(f32[4,8,256]{2,1,0:T(8,128)S(1)} %broadcast_in_dim.22), channel_id=1, replica_groups=mesh['dom_0'=4,'dom_1'=4,'dom_2'=2,'dim'=4] {'dim'}, dimensions={0} | all-to-all | bytes 65536 | tf_op jit(solution)/shard_map/all_to_all | solution.py:33
  211.9 9.7 %all-reduce.12 = f32[4]{0:T(128)S(1)} all-reduce(f32[4]{0:T(128)S(1)} %dynamic-update-slice.12), channel_id=1, replica_groups=mesh['dom_0'=4,'dom_1'=4,'dom_2'=2,'dim'=4] {'dom_0'}, use_global_device_ids=true, to_apply=%add.12 | all-reduce | flops 4 | bytes 32
  223.6 7.7 %all-reduce.13 = f32[4]{0:T(128)S(1)} all-reduce(f32[4]{0:T(128)S(1)} %dynamic-update-slice.13), channel_id=1, replica_groups=mesh['dom_0'=4,'dom_1'=4,'dom_2'=2,'dim'=4] {'dom_1'}, use_global_device_ids=true, to_apply=%add.13 | all-reduce | flops 4 | bytes 32
  237.7 8.9 %all-reduce.15 = f32[4]{0:T(128)S(1)} all-reduce(f32[4]{0:T(128)S(1)} %dynamic-update-slice.15), channel_id=1, replica_groups=mesh['dom_0'=4,'dom_1'=4,'dom_2'=2,'dim'=4] {'dim'}, use_global_device_ids=true, to_apply=%add.15 | all-reduce | flops 4 | bytes 32
  247.9 7.8 %all_to_all.88 = f32[4,8,256]{2,1,0:T(8,128)S(1)} all-to-all(f32[4,8,256]{2,1,0:T(8,128)S(1)} %broadcast_in_dim.23), channel_id=1, replica_groups=mesh['dom_0'=4,'dom_1'=4,'dom_2'=2,'dim'=4] {'dim'}, dimensions={0} | all-to-all | bytes 65536 | tf_op jit(solution)/shard_map/all_to_all | solution.py:33
  256.9 23.8 %all-gather.1 = f32[32,2,2064]{2,1,0:T(2,128)S(1)} all-gather(f32[1,2,2064]{2,1,0:T(2,128)S(1)} %maximum_bitcast_fusion.1), channel_id=1, replica_groups=mesh['dom_0'=4,'dom_1'=4,'dom_2'=2,'dim'=4] {'dom_0','dom_1','dom_2'}, dimensions={0}, use_global_device_ids=true | all-gather | bytes 544896 | tf_op jit(solution)/shard_map/all_gather | solution.py:42
  283.0 11.4 %all_to_all.90 = f32[4,1,24592]{2,1,0:T(1,128)S(1)} all-to-all(f32[4,1,24592]{2,1,0:T(1,128)S(1)} %broadcast_in_dim.24), channel_id=1, replica_groups=mesh['dom_0'=4,'dom_1'=4,'dom_2'=2,'dim'=4] {'dim'}, dimensions={0} | all-to-all | bytes 786944 | tf_op jit(solution)/shard_map/all_to_all | solution.py:33
  322.5 8.9 %all-reduce.36 = (f32[4]{0:T(128)S(1)}, f32[4]{0:T(128)S(1)}, f32[4]{0:T(128)S(1)}) all-reduce(f32[4]{0:T(128)S(1)} %dynamic-update-slice.16, f32[4]{0:T(128)S(1)} %dynamic-update-slice.20, f32[4]{0:T(128)S(1)} %dynamic-update-slice.24), channel_id=1, replica_groups=mesh['dom_0'=4,'dom_1'=4,'dom_2'=2,'dim'=4] {'dom_0'}, use_global_device_ids=true, to_apply=%add.16 | all-reduce | flops 12 | bytes 96
  337.3 9.8 %all-reduce.34 = (f32[4]{0:T(128)S(1)}, f32[4]{0:T(128)S(1)}, f32[4]{0:T(128)S(1)}) all-reduce(f32[4]{0:T(128)S(1)} %dynamic-update-slice.17, f32[4]{0:T(128)S(1)} %dynamic-update-slice.21, f32[4]{0:T(128)S(1)} %dynamic-update-slice.25), channel_id=1, replica_groups=mesh['dom_0'=4,'dom_1'=4,'dom_2'=2,'dim'=4] {'dom_1'}, use_global_device_ids=true, to_apply=%add.17 | all-reduce | flops 12 | bytes 96
  361.4 8.9 %all-reduce.32 = (f32[4]{0:T(128)S(1)}, f32[4]{0:T(128)S(1)}, f32[4]{0:T(128)S(1)}) all-reduce(f32[4]{0:T(128)S(1)} %dynamic-update-slice.19, f32[4]{0:T(128)S(1)} %dynamic-update-slice.23, f32[4]{0:T(128)S(1)} %dynamic-update-slice.27), channel_id=1, replica_groups=mesh['dom_0'=4,'dom_1'=4,'dom_2'=2,'dim'=4] {'dim'}, use_global_device_ids=true, to_apply=%add.19 | all-reduce | flops 12 | bytes 96
  376.3 7.8 %all_to_all.91 = f32[4,8,256]{2,1,0:T(8,128)S(1)} all-to-all(f32[4,8,256]{2,1,0:T(8,128)S(1)} %broadcast_in_dim.26), channel_id=1, replica_groups=mesh['dom_0'=4,'dom_1'=4,'dom_2'=2,'dim'=4] {'dim'}, dimensions={0} | all-to-all | bytes 65536 | tf_op jit(solution)/shard_map/all_to_all | solution.py:33
  399.6 7.7 %all-reduce.28 = f32[4]{0:T(128)S(1)} all-reduce(f32[4]{0:T(128)S(1)} %dynamic-update-slice.28), channel_id=1, replica_groups=mesh['dom_0'=4,'dom_1'=4,'dom_2'=2,'dim'=4] {'dom_0'}, use_global_device_ids=true, to_apply=%add.28 | all-reduce | flops 4 | bytes 32
  409.3 9.7 %all-reduce.29 = f32[4]{0:T(128)S(1)} all-reduce(f32[4]{0:T(128)S(1)} %dynamic-update-slice.29), channel_id=1, replica_groups=mesh['dom_0'=4,'dom_1'=4,'dom_2'=2,'dim'=4] {'dom_1'}, use_global_device_ids=true, to_apply=%add.29 | all-reduce | flops 4 | bytes 32
  425.5 8.9 %all-reduce.31 = f32[4]{0:T(128)S(1)} all-reduce(f32[4]{0:T(128)S(1)} %dynamic-update-slice.31), channel_id=1, replica_groups=mesh['dom_0'=4,'dom_1'=4,'dom_2'=2,'dim'=4] {'dim'}, use_global_device_ids=true, to_apply=%add.31 | all-reduce | flops 4 | bytes 32
  (254 shorter events, 178.3 us)
Async XLA Ops:
  1.3 10.8 %all-to-all-start = ((f32[4,8,256]{2,1,0:T(8,128)}), f32[4,8,256]{2,1,0:T(8,128)S(1)}, u32[]{:S(2)}, u32[]{:S(2)}) async-start(f32[4,8,256]{2,1,0:T(8,128)} %broadcast_in_dim.18), calls=%async_computation | async-start | bytes 65536 | tf_op jit(solution)/shard_map/all_to_all | solution.py:33
  12.1 8.9 %all-to-all-start.1 = ((bf16[8,16,256]{2,1,0:T(8,128)(2,1)}), bf16[8,16,256]{2,1,0:T(8,128)(2,1)S(1)}, u32[]{:S(2)}, u32[]{:S(2)}) async-start(bf16[8,16,256]{2,1,0:T(8,128)(2,1)} %param.4), calls=%async_computation.1 | async-start | bytes 131072 | tf_op jit(solution)/shard_map/all_to_all | solution.py:121
  49.9 12.3 %all-to-all-start.2 = ((f32[4,1,24592]{2,1,0:T(1,128)}), f32[4,1,24592]{2,1,0:T(1,128)S(1)}, u32[]{:S(2)}, u32[]{:S(2)}) async-start(f32[4,1,24592]{2,1,0:T(1,128)} %broadcast_in_dim.19), calls=%async_computation.2 | async-start | bytes 790528 | tf_op jit(solution)/shard_map/all_to_all | solution.py:33
  63.3 8.7 %all-to-all-start.3 = ((f32[4,8,256]{2,1,0:T(8,128)}), f32[4,8,256]{2,1,0:T(8,128)S(1)}, u32[]{:S(2)}, u32[]{:S(2)}) async-start(f32[4,8,256]{2,1,0:T(8,128)} %broadcast_in_dim.20), calls=%async_computation.3 | async-start | bytes 65536 | tf_op jit(solution)/shard_map/all_to_all | solution.py:33
  75.3 5.9 %copy-start.4 = (u32[128]{0:T(128)S(1)}, u32[128]{0:T(128)}, u32[]{:S(2)}) copy-start(u32[128]{0:T(128)} %constant.53) | copy-start | bytes 1540
  75.3 33.8 %all-to-all-start.4 = ((bf16[32,2,16,1024]{3,1,2,0:T(2,128)(2,1)}), bf16[32,2,16,1024]{3,1,2,0:T(2,128)(2,1)S(1)}, u32[]{:S(2)}, u32[]{:S(2)}) async-start(bf16[32,2,16,1024]{3,1,2,0:T(2,128)(2,1)} %broadcast_in_dim.21), calls=%async_computation.4 | async-start | bytes 4194304 | tf_op jit(solution)/shard_map/all_to_all | solution.py:33
  115.2 13.1 %copy-start = (f32[8,256]{1,0:T(8,128)S(1)}, f32[8,256]{1,0:T(8,128)}, u32[]{:S(2)}) copy-start(f32[8,256]{1,0:T(8,128)} %param.3) | copy-start | bytes 24580
  115.2 18.0 %copy-start.3 = (u32[128]{0:T(128)S(1)}, u32[128]{0:T(128)}, u32[]{:S(2)}) copy-start(u32[128]{0:T(128)} %constant.58) | copy-start | bytes 1540
  115.3 33.0 %copy-start.2 = (u32[128]{0:T(128)S(1)}, u32[128]{0:T(128)}, u32[]{:S(2)}) copy-start(u32[128]{0:T(128)} %constant.63) | copy-start | bytes 1540
  115.3 49.3 %copy-start.1 = (u32[128]{0:T(128)S(1)}, u32[128]{0:T(128)}, u32[]{:S(2)}) copy-start(u32[128]{0:T(128)} %constant.68) | copy-start | bytes 1540
  119.7 8.7 %all-to-all-start.5 = ((f32[4,8,256]{2,1,0:T(8,128)}), f32[4,8,256]{2,1,0:T(8,128)S(1)}, u32[]{:S(2)}, u32[]{:S(2)}) async-start(f32[4,8,256]{2,1,0:T(8,128)} %bitcast.23), calls=%async_computation.5 | async-start | bytes 65536 | tf_op jit(solution)/shard_map/all_to_all | solution.py:69
  201.2 8.7 %all-to-all-start.7 = ((f32[4,8,256]{2,1,0:T(8,128)}), f32[4,8,256]{2,1,0:T(8,128)S(1)}, u32[]{:S(2)}, u32[]{:S(2)}) async-start(f32[4,8,256]{2,1,0:T(8,128)} %bitcast.36), calls=%async_computation.7 | async-start | bytes 65536 | tf_op jit(solution)/shard_map/all_to_all | solution.py:69
  295.5 8.7 %all-to-all-start.10 = ((f32[4,8,256]{2,1,0:T(8,128)}), f32[4,8,256]{2,1,0:T(8,128)S(1)}, u32[]{:S(2)}, u32[]{:S(2)}) async-start(f32[4,8,256]{2,1,0:T(8,128)} %broadcast_in_dim.25), calls=%async_computation.10 | async-start | bytes 65536 | tf_op jit(solution)/shard_map/all_to_all | solution.py:33
  308.9 8.7 %all-to-all-start.11 = ((f32[4,8,256]{2,1,0:T(8,128)}), f32[4,8,256]{2,1,0:T(8,128)S(1)}, u32[]{:S(2)}, u32[]{:S(2)}) async-start(f32[4,8,256]{2,1,0:T(8,128)} %bitcast.59), calls=%async_computation.11 | async-start | bytes 65536 | tf_op jit(solution)/shard_map/all_to_all | solution.py:69
  388.9 8.7 %all-to-all-start.13 = ((f32[4,8,256]{2,1,0:T(8,128)}), f32[4,8,256]{2,1,0:T(8,128)S(1)}, u32[]{:S(2)}, u32[]{:S(2)}) async-start(f32[4,8,256]{2,1,0:T(8,128)} %bitcast.72), calls=%async_computation.13 | async-start | bytes 65536 | tf_op jit(solution)/shard_map/all_to_all | solution.py:69
